TPU v7x, 32 devices: a whole 2x2x4 slice. The times are simulated.
32 devices in a mesh: parts: 2 (over y), gz: 4 (over z), gy: 2 (over x), lc: 2 (over core).
Axes of the slice: x: 2, y: 2, z: 4, core: 2. Of those that a mesh axis runs over, the one named last changes fastest.
Arguments:
- density: float32 [64, 128, 256], P(('parts', 'gz'), 'gy'), parts along dimension 0, may hold values from 0.05 to 1
- void_mask: int32 [64, 128, 256], P(('parts', 'gz'), 'gy'), parts along dimension 0, may hold values 0 or 1
- fixed_mask: int32 [64, 128, 256], P(('parts', 'gz'), 'gy'), parts along dimension 0, may hold values 0 or 1
- displacement: float32 [2, 3, 64, 128, 256], P('lc', None, ('parts', 'gz'), 'gy'), parts along dimension 2, may hold values from -4 to 4
- load_ratio: int32 [4], P('parts'), parts along dimension 0, may hold values from 1 to 8
Outputs:
- gradient: float32 [64, 128, 256], P(('parts', 'gz'), 'gy'), parts along dimension 0
There are 2 independent parts, one for each index of `parts`. A program takes and returns all parts, laid end to end along the dimension named above; each array names one. Nothing has to cross between parts.
All inputs are finite; a program needn't handle non-finite values. No bound on the sum of `void_mask` or of `fixed_mask` on one device may be relied on, other than what follows from the above.
Results may differ from a plain program's by a relative error of at most 0.0001.
Values sent between devices are 32-bit elements; how exact they have to be, the bound alone decides.
A program may use at most 64 MiB of HBM per device.

v0:
```python
import math

import jax
import jax.numpy as jnp
import numpy as np
from jax import lax
from jax.sharding import PartitionSpec as P


def shifted(block, axis, distance):
    devices = range(lax.axis_size(axis))
    route = [(i - distance, i) for i in devices if i - distance in devices]
    return lax.ppermute(block, axis, route)


def extended_2(array, sides, width):
    for axis, dim in sides:
        peers, length = (lax.axis_size(axis), array.shape[dim])
        up = [(i, (i + 1) % peers) for i in range(peers - 1)]
        down = [(j, i) for i, j in up]
        last = lax.slice_in_dim(array, length - width, length, axis=dim)
        first = lax.slice_in_dim(array, 0, width, axis=dim)
        before = lax.ppermute(last, axis, up)
        after = lax.ppermute(first, axis, down)
        array = jnp.concatenate([before, array, after], axis=dim)
    return array


def element_stiffness():
    poisson = 0.3
    factor = 1.0 / ((1.0 + poisson) * (1.0 - 2.0 * poisson))
    material = np.zeros((6, 6))
    material[:3, :3] = poisson
    for index in range(3):
        material[index, index] = 1.0 - poisson
        material[index + 3, index + 3] = 0.5 - poisson
    material = material * factor
    corners = [(first, second, third) for first in (0, 1) for second in (0, 1) for third in (0, 1)]
    points = [0.5 - 0.5 / math.sqrt(3.0), 0.5 + 0.5 / math.sqrt(3.0)]
    stiffness = np.zeros((24, 24))
    for point_x in points:
        for point_y in points:
            for point_z in points:
                strain = np.zeros((6, 24))
                for corner_index, (first, second, third) in enumerate(corners):
                    along_x = point_x if first else 1.0 - point_x
                    along_y = point_y if second else 1.0 - point_y
                    along_z = point_z if third else 1.0 - point_z
                    sign_x = 1.0 if first else -1.0
                    sign_y = 1.0 if second else -1.0
                    sign_z = 1.0 if third else -1.0
                    deriv_x = sign_x * along_y * along_z
                    deriv_y = along_x * sign_y * along_z
                    deriv_z = along_x * along_y * sign_z
                    column = 3 * corner_index
                    strain[0, column] = deriv_x
                    strain[1, column + 1] = deriv_y
                    strain[2, column + 2] = deriv_z
                    strain[3, column] = deriv_y
                    strain[3, column + 1] = deriv_x
                    strain[4, column + 1] = deriv_z
                    strain[4, column + 2] = deriv_y
                    strain[5, column] = deriv_z
                    strain[5, column + 2] = deriv_x
                stiffness = stiffness + 0.125 * strain.T @ material @ strain
    return stiffness


def cone_offsets():
    result = []
    for shift_x in range(-2, 3):
        for shift_y in range(-2, 3):
            for shift_z in range(-2, 3):
                dist_sq = shift_x * shift_x + shift_y * shift_y + shift_z * shift_z
                if dist_sq < 6.25:
                    result.append((shift_x, shift_y, shift_z, 2.5 - math.sqrt(dist_sq)))
    return result


def shift_depth(field, offset):
    if offset == 0:
        return field
    depth = field.shape[-1]
    position = jnp.arange(depth, dtype=jnp.int32) + offset
    keep = ((position >= 0) & (position < depth)).astype(jnp.float32)
    return jnp.roll(field, -offset, axis=field.ndim - 1) * keep


def cone_filter(padded, shape):
    rows_x, rows_y, depth = shape
    total = jnp.zeros(shape, jnp.float32)
    offsets = cone_offsets()
    for along_depth in range(-2, 3):
        moved_field = shift_depth(padded, along_depth)
        for shift_x, shift_y, shift_z, weight in offsets:
            if shift_z == along_depth:
                total = (
                    total
                    + weight
                    * moved_field[
                        2 + shift_x : 2 + shift_x + rows_x, 2 + shift_y : 2 + shift_y + rows_y
                    ]
                )
    return total


def inside(start, count, total):
    position = start + jnp.arange(-2, count + 2, dtype=jnp.int32)
    return ((position >= 0) & (position < total)).astype(jnp.float32)


def shards(density, void_mask, fixed_mask, displacement, load_ratio):
    rows_x, rows_y, depth = density.shape
    gz_rank = lax.axis_index("gz")
    gy_rank = lax.axis_index("gy")
    case_rank = lax.axis_index("lc")
    total_x = rows_x * lax.axis_size("gz")
    total_y = rows_y * lax.axis_size("gy")
    column_mask = inside(gy_rank * rows_y, rows_y, total_y)[None, :, None]
    free = (1 - fixed_mask).astype(jnp.float32)
    moved = displacement[0] * free[None]
    next_layer = shifted(moved[:, 0:1], "gz", -1)
    extended = jnp.concatenate([moved, next_layer], 1)
    next_column = shifted(extended[:, :, 0:1], "gy", -1)
    extended = jnp.concatenate([extended, next_column], 2)
    stiffness = jnp.asarray(element_stiffness(), jnp.float32)

    def one_layer(layer):
        layers = lax.dynamic_slice_in_dim(extended, layer, 2, 1)
        nodes = []
        for first in (0, 1):
            for second in (0, 1):
                plane = layers[:, first, second : second + rows_y]
                nodes.append(plane)
                nodes.append(shift_depth(plane, 1))
        flat = jnp.stack(nodes, 0).reshape(24, rows_y * depth)
        product = jnp.dot(stiffness, flat, precision=lax.Precision.HIGHEST)
        return jnp.sum(flat * product, 0).reshape(rows_y, depth)

    energy = lax.map(one_layer, jnp.arange(rows_x, dtype=jnp.int32))
    ratios = load_ratio.astype(jnp.float32)
    own_ratio = lax.dynamic_index_in_dim(ratios, case_rank, 0, keepdims=False)
    term = own_ratio / jnp.sum(ratios) * energy
    alive = (1 - void_mask).astype(jnp.float32)
    half = rows_x // 2
    half_shape = (half, rows_y, depth)
    start = case_rank * half
    filled = inside(gz_rank * rows_x + start, half, total_x)[:, None, None] * column_mask
    filled = jnp.broadcast_to(filled, (half + 4, rows_y + 4, depth))
    weight_sum = cone_filter(filled, half_shape)
    density_half = lax.dynamic_slice_in_dim(density, start, half, 0)
    alive_half = lax.dynamic_slice_in_dim(alive, start, half, 0)
    padded_design = extended_2(density_half, ((("gz", "lc"), 0), ("gy", 1)), 2)
    physical = cone_filter(padded_design, half_shape) / weight_sum
    scaling = alive_half * (-3.0 * physical * physical * (1.0 - 0.001)) / weight_sum
    weighted = lax.psum_scatter(term, "lc", scatter_dimension=0, tiled=True)
    sensed = scaling * weighted
    padded_sense = extended_2(sensed, ((("gz", "lc"), 0), ("gy", 1)), 2)
    filtered = alive_half * cone_filter(padded_sense, half_shape)
    gradient = lax.all_gather(filtered, "lc", axis=0, tiled=True)
    return gradient


def solution(mesh):
    placed = (
        P(("parts", "gz"), "gy", None),
        P(("parts", "gz"), "gy", None),
        P(("parts", "gz"), "gy", None),
        P("lc", None, ("parts", "gz"), "gy", None),
        P("parts"),
    )
    return jax.shard_map(
        shards,
        mesh=mesh,
        in_specs=placed,
        out_specs=P(("parts", "gz"), "gy", None),
        check_vma=False,
    )
```

profile of v0, /device:TPU:15, one launch (start us, length us, event | category | flops | bytes accessed | tf_op | source)
XLA Modules:
  0.0 183.5 jit_solution(11901146239948684260)
XLA Ops:
  6.5 1.1 subtract_convert_fusion
  7.6 1.6 bitcast_multiply_fusion
  10.0 2.1 %collective-permute-start.4 = (f32[3,1,64,256]{3,2,1,0:T(8,128)}, f32[3,1,64,256]{3,2,1,0:T(8,128)S(1)}, u32[]{:S(2)}, u32[]{:S(2)}) collective-permute-start(f32[3,1,64,256]{3,2,1,0:T(8,128)} %slice.1372), channel_id=1, source_target_pairs={{4,0},{8,4},{12,8},{5,1},{9,5},{13,9},{6,2},{10,6},{14,10},{7,3},{... | collective-permute-start | bytes 589832 | tf_op jit(solution)/shard_map/ppermute | solution.py:13
  12.1 2.9 %collective-permute-start.1 = (f32[2,64,256]{2,1,0:T(8,128)S(1)}, f32[2,64,256]{2,1,0:T(8,128)S(1)}, u32[]{:S(2)}, u32[]{:S(2)}) collective-permute-start(f32[2,64,256]{2,1,0:T(8,128)S(1)} %get-tuple-element.109), channel_id=1, source_target_pairs={{1,0},{4,1},{5,4},{8,5},{9,8},{12,9},{13,12},{3,2},{6,3},{7,6},{10... | collective-permute-start | bytes 393224 | tf_op jit(solution)/shard_map/ppermute | solution.py:24
  14.9 3.1 %collective-permute-start = (f32[2,64,256]{2,1,0:T(8,128)S(1)}, f32[2,64,256]{2,1,0:T(8,128)S(1)}, u32[]{:S(2)}, u32[]{:S(2)}) collective-permute-start(f32[2,64,256]{2,1,0:T(8,128)S(1)} %get-tuple-element.108), channel_id=1, source_target_pairs={{0,1},{1,4},{4,5},{5,8},{8,9},{9,12},{12,13},{2,3},{3,6},{6,7},{7,... | collective-permute-start | bytes 393224 | tf_op jit(solution)/shard_map/ppermute | solution.py:23
  20.4 2.2 %collective-permute-start.3 = (f32[8,2,256]{2,1,0:T(2,128)S(1)}, f32[8,2,256]{2,1,0:T(2,128)S(1)}, u32[]{:S(2)}, u32[]{:S(2)}) collective-permute-start(f32[8,2,256]{2,1,0:T(2,128)S(1)} %get-tuple-element.107), channel_id=1, source_target_pairs={{2,0},{3,1},{6,4},{7,5},{10,8},{11,9},{14,12},{15,13},{18,16},{19,... | collective-permute-start | bytes 49160 | tf_op jit(solution)/shard_map/ppermute | solution.py:24
  22.6 1.3 collective-permute-start.2
  25.8 1.2 collective-permute-done.2
  27.1 1.0 fusion.262
  28.2 1.0 fusion.263
  29.2 2.8 %collective-permute-start.5 = (f32[3,9,1,256]{3,2,1,0:T(1,128)S(1)}, f32[3,9,1,256]{3,2,1,0:T(1,128)S(1)}, u32[]{:S(2)}, u32[]{:S(2)}) collective-permute-start(f32[3,9,1,256]{3,2,1,0:T(1,128)S(1)} %pad_maximum_fusion.9), channel_id=1, source_target_pairs={{2,0},{3,1},{6,4},{7,5},{10,8},{11,9},{14,12},{15,13},{18,16},{19,... | collective-permute-start | bytes 82952 | tf_op jit(solution)/shard_map/ppermute | solution.py:13
  32.0 1.1 maximum_maximum_fusion
  33.2 1.5 pad_maximum_fusion
  34.7 93.3 %while.11 = (s32[]{:T(128)}, f32[8,64,256]{2,1,0:T(8,128)}, s32[8]{0:T(128)S(1)}, f32[3,9,65,256]{3,2,1,0:T(8,128)}, s32[]{:T(128)}, /*index=5*/s32[]{:T(128)}, s32[]{:T(128)}, s32[]{}, f32[24,24]{1,0:T(8,128)S(1)}) while((s32[]{:T(128)}, f32[8,64,256]{2,1,0:T(8,128)}, s32[8]{0:T(128)S(1)}, f32[3,9,65,256]{3,2,1,0:T(8,128)}, ...), condition=%wide.region_3.4_spmd.clone, body=%wide.region_1.0_spmd.sunk.clone.sunk | while | flops 114410760 | bytes 11738579 | solution.py:140
  38.2 1.3 dynamic-slice_bitcast_fusion.5
  39.8 1.0 bitcast_dynamic-update-slice_fusion.9
  40.9 1.0 bitcast_dynamic-update-slice_fusion.10
  42.2 1.0 bitcast_dynamic-update-slice_fusion.11
  44.1 1.6 fusion.281
  49.8 1.3 dynamic-slice_bitcast_fusion.5
  51.5 1.0 bitcast_dynamic-update-slice_fusion.9
  52.6 1.0 bitcast_dynamic-update-slice_fusion.10
  53.8 1.0 bitcast_dynamic-update-slice_fusion.11
  55.8 1.6 fusion.281
  61.5 1.3 dynamic-slice_bitcast_fusion.5
  63.2 1.0 bitcast_dynamic-update-slice_fusion.9
  64.2 1.0 bitcast_dynamic-update-slice_fusion.10
  65.5 1.0 bitcast_dynamic-update-slice_fusion.11
  67.5 1.6 fusion.281
  73.2 1.3 dynamic-slice_bitcast_fusion.5
  74.8 1.0 bitcast_dynamic-update-slice_fusion.9
  75.9 1.0 bitcast_dynamic-update-slice_fusion.10
  77.2 1.0 bitcast_dynamic-update-slice_fusion.11
  79.2 1.6 fusion.281
  84.8 1.3 dynamic-slice_bitcast_fusion.5
  86.5 1.0 bitcast_dynamic-update-slice_fusion.9
  87.6 1.0 bitcast_dynamic-update-slice_fusion.10
  88.8 1.0 bitcast_dynamic-update-slice_fusion.11
  90.8 1.6 fusion.281
  96.5 1.3 dynamic-slice_bitcast_fusion.5
  98.2 1.0 bitcast_dynamic-update-slice_fusion.9
  99.2 1.0 bitcast_dynamic-update-slice_fusion.10
  100.5 1.0 bitcast_dynamic-update-slice_fusion.11
  102.5 1.6 fusion.281
  108.2 1.3 dynamic-slice_bitcast_fusion.5
  109.8 1.0 bitcast_dynamic-update-slice_fusion.9
  112.2 1.0 bitcast_dynamic-update-slice_fusion.11
  114.2 1.6 fusion.281
  119.8 1.3 dynamic-slice_bitcast_fusion.5
  121.5 1.0 bitcast_dynamic-update-slice_fusion.9
  123.8 1.0 bitcast_dynamic-update-slice_fusion.11
  125.8 1.6 fusion.281
  128.1 1.9 %broadcast_multiply_fusion = f32[8,64,256]{2,1,0:T(8,128)} fusion(f32[8,64,256]{2,1,0:T(8,128)} %get-tuple-element.32, f32[]{:T(128)S(6)} %div.11), kind=kLoop, calls=%fused_computation.527 | loop fusion | flops 131072 | bytes 1048580 | tf_op jit(solution)/shard_map/mul | solution.py:143
  131.2 1.6 maximum_multiply_fusion.8
  133.5 8.6 %reduce-scatter.2.cloned.1.call-done = f32[4,64,256]{2,1,0:T(8,128)} async-done(((f32[8,64,256]{2,1,0:T(8,128)}), f32[4,64,256]{2,1,0:T(8,128)}) %reduce-scatter.2.cloned.1.call-update) | async-done | bytes 262160 | tf_op jit(solution)/shard_map/reduce_scatter | solution.py:156
  142.1 9.8 %fusion.8 = f32[4,64,256]{2,1,0:T(8,128)S(1)} fusion(f32[4,64,256]{2,1,0:T(8,128)} %reduce-scatter.2.cloned.1.call-done, f32[8,68,256]{2,1,0:T(8,128)} %get-tuple-element.134, f32[8,68,256]{2,1,0:T(8,128)S(1)} %get-tuple-element.133, f32[2,64,256]{2,1,0:T(8,128)} %copy-done.2, f32[4,64,256]{2,1,0:T(8,128)} %copy-done, f32[2,64,256]{2,1,0:T(8,128)} %copy-done.3, ...), kind=kLoop, calls=%fused_computation.61 | loop fusion | flops 20578304 | bytes 36983812 | tf_op jit(solution)/shard_map/mul | solution.py:157
  151.9 2.1 %collective-permute-start.7 = (f32[2,64,256]{2,1,0:T(8,128)S(1)}, f32[2,64,256]{2,1,0:T(8,128)S(1)}, u32[]{:S(2)}, u32[]{:S(2)}) collective-permute-start(f32[2,64,256]{2,1,0:T(8,128)S(1)} %get-tuple-element.111), channel_id=1, source_target_pairs={{1,0},{4,1},{5,4},{8,5},{9,8},{12,9},{13,12},{3,2},{6,3},{7,6},{10... | collective-permute-start | bytes 393224 | tf_op jit(solution)/shard_map/ppermute | solution.py:24
  154.0 3.5 %collective-permute-start.6 = (f32[2,64,256]{2,1,0:T(8,128)S(1)}, f32[2,64,256]{2,1,0:T(8,128)S(1)}, u32[]{:S(2)}, u32[]{:S(2)}) collective-permute-start(f32[2,64,256]{2,1,0:T(8,128)S(1)} %get-tuple-element.110), channel_id=1, source_target_pairs={{0,1},{1,4},{4,5},{5,8},{8,9},{9,12},{12,13},{2,3},{3,6},{6,7},{7,... | collective-permute-start | bytes 393224 | tf_op jit(solution)/shard_map/ppermute | solution.py:23
  158.2 1.2 collective-permute-done.6
  159.4 2.2 %collective-permute-start.9 = (f32[8,2,256]{2,1,0:T(2,128)S(1)}, f32[8,2,256]{2,1,0:T(2,128)S(1)}, u32[]{:S(2)}, u32[]{:S(2)}) collective-permute-start(f32[8,2,256]{2,1,0:T(2,128)S(1)} %get-tuple-element.103), channel_id=1, source_target_pairs={{2,0},{3,1},{6,4},{7,5},{10,8},{11,9},{14,12},{15,13},{18,16},{19,... | collective-permute-start | bytes 49160 | tf_op jit(solution)/shard_map/ppermute | solution.py:24
  161.6 1.3 collective-permute-start.8
  162.9 3.2 %collective-permute-done.8 = f32[8,2,256]{2,1,0:T(2,128)S(1)} collective-permute-done((f32[8,2,256]{2,1,0:T(2,128)S(1)}, f32[8,2,256]{2,1,0:T(2,128)S(1)}, u32[]{:S(2)}, u32[]{:S(2)}) %collective-permute-start.8) | collective-permute-done | bytes 16416 | tf_op jit(solution)/shard_map/ppermute | solution.py:23
  168.5 2.8 %fusion.88 = f32[4,64,256]{2,1,0:T(8,128)S(1)} fusion(f32[8,68,256]{2,1,0:T(8,128)S(1)} %maximum_multiply_fusion.15, f32[8,68,256]{2,1,0:T(8,128)S(1)} %maximum_multiply_fusion.14, f32[2,64,256]{2,1,0:T(8,128)S(1)} %collective-permute-done.7, f32[4,64,256]{2,1,0:T(8,128)S(1)} %fusion.8, f32[2,64,256]{2,1,0:T(8,128)S(1)} %collective-permute-done.6, ...), kind=kLoop, calls=%fused_computation.142 | loop fusion | flops 11010048 | bytes 20971524 | tf_op jit(solution)/shard_map/mul | solution.py:159
  171.3 4.6 %all_gather.3 = f32[8,64,256]{2,1,0:T(8,128)S(1)} all-gather(f32[4,64,256]{2,1,0:T(8,128)S(1)} %fusion.88), channel_id=1, replica_groups=mesh['parts'=2,'gz'=4,'gy'=2,'lc'=2] {'lc'}, dimensions={0}, use_global_device_ids=true | all-gather | bytes 786432 | tf_op jit(solution)/shard_map/all_gather | solution.py:160
  (182 shorter events, 42.4 us)
Async XLA Ops:
  6.5 135.6 %reduce-scatter.2.cloned.1.call-start = ((), (), s32[]{:S(2)}) async-start(), calls=%async_computation.1 | async-start | bytes 786432 | tf_op jit(solution)/shard_map/reduce_scatter | solution.py:156
  7.6 4.4 %copy-start.8 = (f32[8,64,256]{2,1,0:T(8,128)S(1)}, f32[8,64,256]{2,1,0:T(8,128)}, u32[]{:S(2)}) copy-start(f32[8,64,256]{2,1,0:T(8,128)} %param.8) | copy-start | bytes 1572868
  7.6 12.0 %copy-start.10 = (s32[2]{0:T(128)S(1)}, s32[2]{0:T(128)}, u32[]{:S(2)}) copy-start(s32[2]{0:T(128)} %param.12) | copy-start | bytes 28
  10.0 19.2 %collective-permute-start.4 = (f32[3,1,64,256]{3,2,1,0:T(8,128)}, f32[3,1,64,256]{3,2,1,0:T(8,128)S(1)}, u32[]{:S(2)}, u32[]{:S(2)}) collective-permute-start(f32[3,1,64,256]{3,2,1,0:T(8,128)} %slice.1372), channel_id=1, source_target_pairs={{4,0},{8,4},{12,8},{5,1},{9,5},{13,9},{6,2},{10,6},{14,10},{7,3},{... | collective-permute-start | bytes 589832 | tf_op jit(solution)/shard_map/ppermute | solution.py:13
  12.1 8.3 %collective-permute-start.1 = (f32[2,64,256]{2,1,0:T(8,128)S(1)}, f32[2,64,256]{2,1,0:T(8,128)S(1)}, u32[]{:S(2)}, u32[]{:S(2)}) collective-permute-start(f32[2,64,256]{2,1,0:T(8,128)S(1)} %get-tuple-element.109), channel_id=1, source_target_pairs={{1,0},{4,1},{5,4},{8,5},{9,8},{12,9},{13,12},{3,2},{6,3},{7,6},{10... | collective-permute-start | bytes 393224 | tf_op jit(solution)/shard_map/ppermute | solution.py:24
  14.9 5.4 %collective-permute-start = (f32[2,64,256]{2,1,0:T(8,128)S(1)}, f32[2,64,256]{2,1,0:T(8,128)S(1)}, u32[]{:S(2)}, u32[]{:S(2)}) collective-permute-start(f32[2,64,256]{2,1,0:T(8,128)S(1)} %get-tuple-element.108), channel_id=1, source_target_pairs={{0,1},{1,4},{4,5},{5,8},{8,9},{9,12},{12,13},{2,3},{3,6},{6,7},{7,... | collective-permute-start | bytes 393224 | tf_op jit(solution)/shard_map/ppermute | solution.py:23
  20.2 11.8 %copy-start = (f32[4,64,256]{2,1,0:T(8,128)}, f32[4,64,256]{2,1,0:T(8,128)S(1)}, u32[]{:S(2)}) copy-start(f32[4,64,256]{2,1,0:T(8,128)S(1)} %constant_dynamic-slice_fusion.2) | copy-start | bytes 786436
  20.4 11.6 %copy-start.2 = (f32[2,64,256]{2,1,0:T(8,128)}, f32[2,64,256]{2,1,0:T(8,128)S(1)}, u32[]{:S(2)}) copy-start(f32[2,64,256]{2,1,0:T(8,128)S(1)} %collective-permute-done.1) | copy-start | bytes 393220
  20.4 11.7 %copy-start.3 = (f32[2,64,256]{2,1,0:T(8,128)}, f32[2,64,256]{2,1,0:T(8,128)S(1)}, u32[]{:S(2)}) copy-start(f32[2,64,256]{2,1,0:T(8,128)S(1)} %collective-permute-done) | copy-start | bytes 393220
  20.4 5.4 %collective-permute-start.3 = (f32[8,2,256]{2,1,0:T(2,128)S(1)}, f32[8,2,256]{2,1,0:T(2,128)S(1)}, u32[]{:S(2)}, u32[]{:S(2)}) collective-permute-start(f32[8,2,256]{2,1,0:T(2,128)S(1)} %get-tuple-element.107), channel_id=1, source_target_pairs={{2,0},{3,1},{6,4},{7,5},{10,8},{11,9},{14,12},{15,13},{18,16},{19,... | collective-permute-start | bytes 49160 | tf_op jit(solution)/shard_map/ppermute | solution.py:24
  22.6 4.5 %collective-permute-start.2 = (f32[8,2,256]{2,1,0:T(2,128)S(1)}, f32[8,2,256]{2,1,0:T(2,128)S(1)}, u32[]{:S(2)}, u32[]{:S(2)}) collective-permute-start(f32[8,2,256]{2,1,0:T(2,128)S(1)} %get-tuple-element.106), channel_id=1, source_target_pairs={{0,2},{1,3},{4,6},{5,7},{8,10},{9,11},{12,14},{13,15},{16,18},{17,... | collective-permute-start | bytes 49160 | tf_op jit(solution)/shard_map/ppermute | solution.py:23
  29.2 4.0 %collective-permute-start.5 = (f32[3,9,1,256]{3,2,1,0:T(1,128)S(1)}, f32[3,9,1,256]{3,2,1,0:T(1,128)S(1)}, u32[]{:S(2)}, u32[]{:S(2)}) collective-permute-start(f32[3,9,1,256]{3,2,1,0:T(1,128)S(1)} %pad_maximum_fusion.9), channel_id=1, source_target_pairs={{2,0},{3,1},{6,4},{7,5},{10,8},{11,9},{14,12},{15,13},{18,16},{19,... | collective-permute-start | bytes 82952 | tf_op jit(solution)/shard_map/ppermute | solution.py:13
  33.2 1.5 copy-start.9
  130.1 1.1 copy-start.1
  131.2 1.7 copy-start.4
  131.2 1.7 copy-start.5
  131.2 1.7 copy-start.6
  151.9 6.3 %collective-permute-start.7 = (f32[2,64,256]{2,1,0:T(8,128)S(1)}, f32[2,64,256]{2,1,0:T(8,128)S(1)}, u32[]{:S(2)}, u32[]{:S(2)}) collective-permute-start(f32[2,64,256]{2,1,0:T(8,128)S(1)} %get-tuple-element.111), channel_id=1, source_target_pairs={{1,0},{4,1},{5,4},{8,5},{9,8},{12,9},{13,12},{3,2},{6,3},{7,6},{10... | collective-permute-start | bytes 393224 | tf_op jit(solution)/shard_map/ppermute | solution.py:24
  154.0 5.4 %collective-permute-start.6 = (f32[2,64,256]{2,1,0:T(8,128)S(1)}, f32[2,64,256]{2,1,0:T(8,128)S(1)}, u32[]{:S(2)}, u32[]{:S(2)}) collective-permute-start(f32[2,64,256]{2,1,0:T(8,128)S(1)} %get-tuple-element.110), channel_id=1, source_target_pairs={{0,1},{1,4},{4,5},{5,8},{8,9},{9,12},{12,13},{2,3},{3,6},{6,7},{7,... | collective-permute-start | bytes 393224 | tf_op jit(solution)/shard_map/ppermute | solution.py:23
  159.4 3.5 %collective-permute-start.9 = (f32[8,2,256]{2,1,0:T(2,128)S(1)}, f32[8,2,256]{2,1,0:T(2,128)S(1)}, u32[]{:S(2)}, u32[]{:S(2)}) collective-permute-start(f32[8,2,256]{2,1,0:T(2,128)S(1)} %get-tuple-element.103), channel_id=1, source_target_pairs={{2,0},{3,1},{6,4},{7,5},{10,8},{11,9},{14,12},{15,13},{18,16},{19,... | collective-permute-start | bytes 49160 | tf_op jit(solution)/shard_map/ppermute | solution.py:24
  161.6 4.5 %collective-permute-start.8 = (f32[8,2,256]{2,1,0:T(2,128)S(1)}, f32[8,2,256]{2,1,0:T(2,128)S(1)}, u32[]{:S(2)}, u32[]{:S(2)}) collective-permute-start(f32[8,2,256]{2,1,0:T(2,128)S(1)} %get-tuple-element.102), channel_id=1, source_target_pairs={{0,2},{1,3},{4,6},{5,7},{8,10},{9,11},{12,14},{13,15},{16,18},{17,... | collective-permute-start | bytes 49160 | tf_op jit(solution)/shard_map/ppermute | solution.py:23
  167.4 1.0 copy-start.7
Sparse Core Ops, SparseCore 0:
  130.1 11.9 reduce-scatter.1
where the time goes:
time: 185 us; the launch traced here: 184 us
  local copies, waits for them, and re-layouts  67.7 us (37%)
  other arithmetic  29.2 us (16%)
  starting transfers between devices  23.3 us (13%)
  loops' own time  16.1 us (9%)
  waiting for transfers between devices  15.1 us (8%)
  between operations  15.1 us (8%)
  matrix products  12.4 us (7%)
  blocking collectives  4.59 us (2%)
    while x40, local copies, waits for them, and re-layouts  38 us
    another operation x1, loops' own time, shards(): energy = lax.map(one_layer, jnp.arange(rows_x, dtype=jnp.int32))  16.1 us
    dot_general x8, matrix products, one_layer(): product = jnp.dot(stiffness, flat, precision=lax.Precision.HIGHEST)  12.4 us
    squeeze x8, local copies, waits for them, and re-layouts, one_layer(): plane = layers[:, first, second:second + rows_y]  10.7 us
    mul x1, other arithmetic, shards(): sensed = scaling * weighted  9.76 us
    ppermute x4, starting transfers between devices, extended_2(): after = lax.ppermute(first, axis, down)  9.27 us
    ppermute x4, starting transfers between devices, extended_2(): before = lax.ppermute(last, axis, up)  9.18 us
    reduce_scatter x1, waiting for transfers between devices, shards(): weighted = lax.psum_scatter(term, 'lc', scatter_dimension=0, tiled=True)  8.64 us
  transfers between devices with their start and end apart: 11, of which 6 were waited for; matrix products, arithmetic and copies ran while one was open for 5% of the time, Pallas kernels for 0%

commit v1 on v0

v1 whole, which is shorter than its diff:
```python
import math

import jax
import jax.numpy as jnp
from jax import lax
from jax.experimental import pallas as pl
from jax.experimental.pallas import tpu as pltpu
from jax.sharding import PartitionSpec as P

MESH = pl.DeviceIdType.MESH
POISSON = 0.3
FACTOR = 1.0 / ((1.0 + POISSON) * (1.0 - 2.0 * POISSON))
LAMBDA = POISSON * FACTOR
SHEAR = (0.5 - POISSON) * FACTOR
W = [2.5 - math.sqrt(d) for d in range(7)]
N_COPIES = 19


def layer_classes(q0, q1, q2, q4, q5):
    p0 = W[0] * q0 + W[1] * q1 + W[2] * q2 + W[4] * q4 + W[5] * q5
    p1 = W[1] * q0 + W[2] * q1 + W[3] * q2 + W[5] * q4 + W[6] * q5
    p2 = W[4] * q0 + W[5] * q1 + W[6] * q2
    return p0, p1, p2


def lane_index(shape):
    return lax.broadcasted_iota(jnp.int32, shape, len(shape) - 1)


def lane_pair(field, step):
    depth = field.shape[-1]
    lane = lane_index(field.shape)
    after = jnp.where(lane < depth - step, pltpu.roll(field, depth - step, 1), 0.0)
    before = jnp.where(lane >= step, pltpu.roll(field, step, 1), 0.0)
    return after + before


def cone_tile(ref, layer, row):
    f = [ref[layer + k, pl.ds(row, 24), :] for k in range(5)]
    x0, x1, x2 = f[2], f[1] + f[3], f[0] + f[4]

    def pair(t, step):
        return (pltpu.roll(t, step, 0) + pltpu.roll(t, 24 - step, 0))[8:16]

    q0 = x0[8:16]
    q1 = x1[8:16] + pair(x0, 1)
    q2 = pair(x1, 1)
    q4 = x2[8:16] + pair(x0, 2)
    q5 = pair(x2, 1) + pair(x1, 2)
    p0, p1, p2 = layer_classes(q0, q1, q2, q4, q5)
    return p0 + lane_pair(p1, 1) + lane_pair(p2, 2)


def present(position, total, step):
    before = (position >= step).astype(jnp.float32)
    return before + (position + step < total).astype(jnp.float32)


def weight_tile(layer, layers, row, rows, depth):
    shape = (8, depth)
    sub = lax.broadcasted_iota(jnp.int32, shape, 0) + row
    spot = jnp.full(shape, layer, jnp.int32)
    nx1, nx2 = present(spot, layers, 1), present(spot, layers, 2)
    ny1, ny2 = present(sub, rows, 1), present(sub, rows, 2)
    one = jnp.ones(shape, jnp.float32)
    p0, p1, p2 = layer_classes(one, nx1 + ny1, nx1 * ny1, nx2 + ny2, nx2 * ny1 + nx1 * ny2)
    lane = lane_index(shape)
    return p0 + present(lane, depth, 1) * p1 + present(lane, depth, 2) * p2


def node_modes(ref, comp, layer, row):
    t = ref[comp, layer, pl.ds(row, 16), :]
    depth = t.shape[-1]
    tn = jnp.where(lane_index(t.shape) < depth - 1, pltpu.roll(t, depth - 1, 1), 0.0)
    s, d = t + tn, tn - t
    s0, d0 = s[0:8], d[0:8]
    s1, d1 = pltpu.roll(s, 15, 0)[0:8], pltpu.roll(d, 15, 0)[0:8]
    return s0 + s1, d0 + d1, s1 - s0, d1 - d0


def energy_tile(ref, layer, row):
    modes = []
    for comp in range(3):
        a = node_modes(ref, comp, layer, row)
        b = node_modes(ref, comp, layer + 1, row)
        modes.append(
            {
                "x": b[0] - a[0],
                "z": a[1] + b[1],
                "y": a[2] + b[2],
                "yz": a[3] + b[3],
                "xz": b[1] - a[1],
                "xy": b[2] - a[2],
                "xyz": b[3] - a[3],
            }
        )
    u, v, w = modes
    sq = lambda t: t * t
    trace = sq(u["x"] + v["y"] + w["z"])
    linear = sq(v["xy"] + w["xz"]) + sq(u["xy"] + w["yz"]) + sq(u["xz"] + v["yz"])
    normal = sq(u["x"]) + sq(v["y"]) + sq(w["z"])
    bend = sq(u["xy"]) + sq(u["xz"]) + sq(v["xy"]) + sq(v["yz"]) + sq(w["yz"]) + sq(w["xz"])
    shear = sq(u["y"] + v["x"]) + sq(u["z"] + w["x"]) + sq(v["z"] + w["y"])
    twist = sq(u["yz"] + v["xz"]) + sq(u["yz"] + w["xy"]) + sq(v["xz"] + w["xy"])
    cubic = sq(u["xyz"]) + sq(v["xyz"]) + sq(w["xyz"])
    return (1.0 / 16.0) * (
        LAMBDA * trace
        + (LAMBDA / 3.0) * linear
        + (2.0 * SHEAR) * normal
        + SHEAR * (bend + shear)
        + (SHEAR / 3.0) * twist
        + ((LAMBDA + 4.0 * SHEAR) / 9.0) * cubic
    )


def kernel(
    ratio, density, void, fixed, disp, out,
    moved, fix, col_s, col_r, cor_s, cor_r, dens, dead, scale, energy, other, sens, grad,
    local, send, recv,
):
    layers, rows, depth = density.shape
    half = layers // 2
    tiles = rows // 8
    r, c, h = lax.axis_index("gz"), lax.axis_index("gy"), lax.axis_index("lc")
    nr, nc = lax.axis_size("gz"), lax.axis_size("gy")
    dz = 1 - 2 * h
    mid = pl.ds(8, rows)
    low, high = pl.ds(0, 8), pl.ds(rows + 8, 8)

    def there(step_z, step_y):
        z, y = r + step_z, c + step_y
        return (z >= 0) & (z < nr) & (y >= 0) & (y < nc)

    def remote(index, src, dst, step_z, step_y, core):
        copy = pltpu.make_async_remote_copy(
            src_ref=src, dst_ref=dst, send_sem=send.at[index], recv_sem=recv.at[index],
            device_id={"gz": r + step_z, "gy": c + step_y, "lc": core}, device_id_type=MESH,
        )
        goes, comes = there(step_z, step_y), there(-step_z, -step_y)
        return copy, goes, comes

    def start(entry):
        copy, goes, _ = entry
        pl.when(goes)(copy.start)

    def arrive(entry):
        copy, _, comes = entry
        pl.when(comes)(copy.wait_recv)

    def left(entry):
        copy, goes, _ = entry
        pl.when(goes)(copy.wait_send)

    l0, b0 = half // 2 * (1 - h), half // 2 * h
    keep = half + 2
    lz, sb = (half + 2) * h, (layers - 2) * (1 - h)
    get_disp = pltpu.make_async_copy(
        disp.at[0], moved.at[:, pl.ds(0, layers), pl.ds(0, rows), :], local.at[0]
    )
    get_fix = pltpu.make_async_copy(fixed, fix, local.at[1])
    get_dens = pltpu.make_async_copy(
        density.at[pl.ds(b0, keep)], dens.at[pl.ds(l0, keep), mid, :], local.at[2]
    )
    get_dead = pltpu.make_async_copy(void.at[pl.ds(half * h, half)], dead, local.at[3])
    for copy in (get_disp, get_fix, get_dens, get_dead):
        copy.start()

    barrier = pltpu.get_barrier_semaphore()
    for step_z in (-1, 0, 1):
        for step_y in (-1, 0, 1):
            for flip in (0, 1):
                if step_z == 0 and step_y == 0 and flip == 0:
                    continue
                core = h if flip == 0 else 1 - h

                @pl.when(there(step_z, step_y))
                def _():
                    pl.semaphore_signal(
                        barrier, inc=1,
                        device_id={"gz": r + step_z, "gy": c + step_y, "lc": core},
                        device_id_type=MESH,
                    )

    span_z = 1 + (r > 0).astype(jnp.int32) + (r < nr - 1).astype(jnp.int32)
    span_y = 1 + (c > 0).astype(jnp.int32) + (c < nc - 1).astype(jnp.int32)
    pl.semaphore_wait(barrier, 2 * span_z * span_y - 1)

    own, edge = pl.ds(b0, keep), pl.ds(sb, 2)
    top, bottom = pl.ds(rows - 8, 8), pl.ds(0, 8)
    near, far = pl.ds(l0, keep), pl.ds(lz, 2)
    dens_copies = [
        remote(0, density.at[edge], dens.at[far, mid, :], dz, 0, h),
        remote(1, density.at[own, top, :], dens.at[near, low, :], 0, 1, h),
        remote(2, density.at[own, bottom, :], dens.at[near, high, :], 0, -1, h),
        remote(3, density.at[edge, top, :], dens.at[far, low, :], dz, 1, h),
        remote(4, density.at[edge, bottom, :], dens.at[far, high, :], dz, -1, h),
    ]

    get_disp.wait()
    get_fix.wait()

    def free_layer(i, _):
        free = (1 - fix[i]).astype(jnp.float32)
        for comp in range(3):
            moved[comp, i, pl.ds(0, rows), :] = moved[comp, i, pl.ds(0, rows), :] * free
        return 0

    lax.fori_loop(0, layers, free_layer, 0)
    for comp in range(3):
        for i in range(layers):
            col_s[comp, i : i + 1, :] = moved[comp, i, 0:1, :]
        cor_s[comp : comp + 1, :] = moved[comp, 0, 0:1, :]
    plane = pl.ds(0, rows)
    send_layer = remote(
        5, moved.at[:, 0, plane, :], moved.at[:, layers, plane, :], -1, 0, h
    )
    send_col = remote(6, col_s, col_r, 0, -1, h)
    send_cor = remote(7, cor_s, cor_r, -1, -1, h)
    for entry in (send_col, send_cor, send_layer):
        start(entry)
    for entry in dens_copies:
        start(entry)

    @pl.when(r == nr - 1)
    def _():
        for comp in range(3):
            moved[comp, layers, plane, :] = jnp.zeros((rows, depth), jnp.float32)

    @pl.when(c == nc - 1)
    def _():
        col_r[...] = jnp.zeros_like(col_r)

    @pl.when(jnp.logical_not(there(1, 1)))
    def _():
        cor_r[...] = jnp.zeros_like(cor_r)

    blank = jnp.zeros((8, depth), jnp.float32)
    for ref in (dens, sens):

        @pl.when(c == 0)
        def _():
            for i in range(half + 4):
                ref[i, low, :] = blank

        @pl.when(c == nc - 1)
        def _():
            for i in range(half + 4):
                ref[i, high, :] = blank

        @pl.when(jnp.logical_not(there(-dz, 0)))
        def _():
            for i in range(2):
                ref[lz + i] = jnp.zeros((rows + 16, depth), jnp.float32)

    arrive(send_col)
    for comp in range(3):
        for i in range(layers):
            moved[comp, i, pl.ds(rows, 1), :] = col_r[comp, i : i + 1, :]

    ratio_sum = ratio[0]
    for case in range(1, ratio.shape[0]):
        ratio_sum = ratio_sum + ratio[case]
    share = jnp.full((8, depth), ratio[h].astype(jnp.float32)) / jnp.full(
        (8, depth), ratio_sum.astype(jnp.float32)
    )

    def energy_layer(i):
        def tile(j, _):
            row = pl.multiple_of(j * 8, 8)
            energy[i, pl.ds(row, 8), :] = share * energy_tile(moved, i, row)
            return 0

        lax.fori_loop(0, tiles, tile, 0)

    def energy_step(k, _):
        energy_layer(lax.rem(k + half * (1 - h), layers - 1))
        return 0

    give = half * (1 - h)
    swap_a = remote(
        8, energy.at[pl.ds(give, half - 1)], other.at[pl.ds(0, half - 1)], 0, 0, 1 - h
    )
    swap_b = remote(
        9, energy.at[pl.ds(give + half - 1, 1)], other.at[pl.ds(half - 1, 1)], 0, 0, 1 - h
    )
    lax.fori_loop(0, half - 1, energy_step, 0)
    start(swap_a)
    lax.fori_loop(half - 1, half, energy_step, 0)
    pl.when(h == 1)(swap_b[0].start)
    lax.fori_loop(half, layers - 1, energy_step, 0)

    get_dens.wait()
    get_dead.wait()
    for entry in dens_copies:
        arrive(entry)

    def scale_step(n, _):
        j, k = n // tiles, lax.rem(n, tiles)
        row = pl.multiple_of(k * 8, 8)
        weights = weight_tile(
            r * layers + half * h + j, nr * layers, c * rows + row, nc * rows, depth
        )
        inverse = 1.0 / weights
        physical = cone_tile(dens, j, row) * inverse
        alive = (1 - dead[j, pl.ds(row, 8), :]).astype(jnp.float32)
        scale[j, pl.ds(row, 8), :] = (
            alive * (-3.0 * (1.0 - 0.001)) * physical * physical * inverse
        )
        return 0

    lax.fori_loop(0, half * tiles, scale_step, 0)

    arrive(send_layer)
    arrive(send_cor)
    for comp in range(3):
        moved[comp, layers, pl.ds(rows, 1), :] = cor_r[comp : comp + 1, :]
    energy_layer(layers - 1)
    pl.when(h == 0)(swap_b[0].start)
    arrive(swap_a)
    arrive(swap_b)

    def sense_step(j, _):
        sens[2 + j, mid, :] = scale[j] * (energy[half * h + j] + other[j])
        return 0

    lax.fori_loop(0, half, sense_step, 0)
    ps, pd = pl.ds(half - (half - 2) * h, 2), pl.ds((half + 2) * h, 2)
    zs, zd = pl.ds(2 + (half - 2) * h, 2), pl.ds((half + 2) * (1 - h), 2)
    rest = pl.ds(2, half)
    last, first = pl.ds(rows, 8), pl.ds(8, 8)
    sense_copies = [
        remote(11, sens.at[zs, mid, :], sens.at[zd, mid, :], -dz, 0, 1 - h),
        remote(10, sens.at[ps, mid, :], sens.at[pd, mid, :], 0, 0, 1 - h),
        remote(16, sens.at[zs, last, :], sens.at[zd, low, :], -dz, 1, 1 - h),
        remote(17, sens.at[zs, first, :], sens.at[zd, high, :], -dz, -1, 1 - h),
        remote(12, sens.at[rest, last, :], sens.at[rest, low, :], 0, 1, h),
        remote(13, sens.at[rest, first, :], sens.at[rest, high, :], 0, -1, h),
        remote(14, sens.at[ps, last, :], sens.at[pd, low, :], 0, 1, 1 - h),
        remote(15, sens.at[ps, first, :], sens.at[pd, high, :], 0, -1, 1 - h),
    ]
    sides = {11: (-dz, 0), 16: (-dz, -1), 17: (-dz, 1)}
    numbers = (11, 10, 16, 17, 12, 13, 14, 15)
    sense_copies = [
        (copy, goes, there(*sides[n]) if n in sides else comes)
        for n, (copy, goes, comes) in zip(numbers, sense_copies)
    ]
    for entry in sense_copies:
        start(entry)
    for entry in sense_copies:
        arrive(entry)

    def filter_step(n, _):
        j, k = n // tiles, lax.rem(n, tiles)
        row = pl.multiple_of(k * 8, 8)
        alive = (1 - dead[j, pl.ds(row, 8), :]).astype(jnp.float32)
        grad[j, pl.ds(row, 8), :] = alive * cone_tile(sens, j, row)
        return 0

    lax.fori_loop(0, half * tiles, filter_step, 0)
    place = pl.ds(half * h, half)
    put = pltpu.make_async_copy(grad, out.at[place], local.at[4])
    give_out = remote(18, grad, out.at[place], 0, 0, 1 - h)
    start(give_out)
    put.start()
    for entry in [*dens_copies, send_layer, send_col, send_cor, swap_a, swap_b, *sense_copies]:
        left(entry)
    left(give_out)
    arrive(give_out)
    put.wait()


def shards(density, void_mask, fixed_mask, displacement, load_ratio):
    layers, rows, depth = density.shape
    half = layers // 2
    f32 = jnp.float32
    hbm = pl.BlockSpec(memory_space=pl.ANY)
    return pl.pallas_call(
        kernel,
        out_shape=jax.ShapeDtypeStruct(density.shape, f32),
        in_specs=[pl.BlockSpec(memory_space=pltpu.SMEM), hbm, hbm, hbm, hbm],
        out_specs=hbm,
        scratch_shapes=[
            pltpu.VMEM((3, layers + 1, rows + 8, depth), f32),
            pltpu.VMEM((layers, rows, depth), jnp.int32),
            pltpu.VMEM((3, layers, depth), f32),
            pltpu.VMEM((3, layers, depth), f32),
            pltpu.VMEM((8, depth), f32),
            pltpu.VMEM((8, depth), f32),
            pltpu.VMEM((half + 4, rows + 16, depth), f32),
            pltpu.VMEM((half, rows, depth), jnp.int32),
            pltpu.VMEM((half, rows, depth), f32),
            pltpu.VMEM((layers, rows, depth), f32),
            pltpu.VMEM((half, rows, depth), f32),
            pltpu.VMEM((half + 4, rows + 16, depth), f32),
            pltpu.VMEM((half, rows, depth), f32),
            pltpu.SemaphoreType.DMA((5,)),
            pltpu.SemaphoreType.DMA((N_COPIES,)),
            pltpu.SemaphoreType.DMA((N_COPIES,)),
        ],
        compiler_params=pltpu.CompilerParams(collective_id=0, has_side_effects=True),
    )(load_ratio, density, void_mask, fixed_mask, displacement)


def solution(mesh):
    placed = (
        P(("parts", "gz"), "gy", None),
        P(("parts", "gz"), "gy", None),
        P(("parts", "gz"), "gy", None),
        P("lc", None, ("parts", "gz"), "gy", None),
        P("parts"),
    )
    return jax.shard_map(
        shards,
        mesh=mesh,
        in_specs=placed,
        out_specs=P(("parts", "gz"), "gy", None),
        check_vma=False,
    )
```

time: 185 us -> 30 us (0.16)
  the two profiles are of different devices: /device:TPU:15 before, /device:TPU:0 now
where the time goes in v1:
time: 30 us; the launch traced here: 29.8 us
  Pallas kernels  27.9 us (93%)
  local copies, waits for them, and re-layouts  1.87 us (6%)
    pallas_call x1, Pallas kernels, shards(): pl.pallas_call(kernel, out_shape=jax.ShapeDtypeStruct(density.shape, f32)...  27.9 us
    unnamed x1, local copies, waits for them, and re-layouts  1.87 us

profile of v1, /device:TPU:0, one launch (start us, length us, event | category | flops | bytes accessed | tf_op | source)
XLA Modules:
  0.0 29.8 jit_solution(9687751654608133206)
XLA Ops:
  0.0 27.9 %shard_map.55 = f32[8,64,256]{2,1,0:T(8,128)} custom-call(s32[2]{0:T(128)} %ratio.1, f32[8,64,256]{2,1,0:T(8,128)} %density.1, s32[8,64,256]{2,1,0:T(8,128)} %void.1, s32[8,64,256]{2,1,0:T(8,128)} %fixed.1, f32[1,3,8,64,256]{4,3,2,1,0:T(8,128)} %disp.1), custom_call_target="tpu_custom_call" | custom-call | tf_op jit(solution)/shard_map/pallas_call | solution.py:377
  28.0 1.9 %copy.7 = f32[8,64,256]{2,1,0:T(8,128)} copy(f32[8,64,256]{2,1,0:T(8,128)} %shard_map.55) | data formatting | bytes 1048576

commit v2 on v1

--- a/solution.py
+++ b/solution.py
@@ -13,7 +13,9 @@
 LAMBDA = POISSON * FACTOR
 SHEAR = (0.5 - POISSON) * FACTOR
 W = [2.5 - math.sqrt(d) for d in range(7)]
-N_COPIES = 19
+N_COPIES = 24
+TALL = 16
+SHORT = 8
 
 
 def layer_classes(q0, q1, q2, q4, q5):
@@ -35,20 +37,25 @@
     return after + before
 
 
-def cone_tile(ref, layer, row):
-    f = [ref[layer + k, pl.ds(row, 24), :] for k in range(5)]
-    x0, x1, x2 = f[2], f[1] + f[3], f[0] + f[4]
+def cone_tiles(ref, layer, row, count):
+    window = TALL + 16
+    f = [ref[layer + k, pl.ds(row, window), :] for k in range(count + 4)]
+    mid = slice(8, 8 + TALL)
 
     def pair(t, step):
-        return (pltpu.roll(t, step, 0) + pltpu.roll(t, 24 - step, 0))[8:16]
-
-    q0 = x0[8:16]
-    q1 = x1[8:16] + pair(x0, 1)
-    q2 = pair(x1, 1)
-    q4 = x2[8:16] + pair(x0, 2)
-    q5 = pair(x2, 1) + pair(x1, 2)
-    p0, p1, p2 = layer_classes(q0, q1, q2, q4, q5)
-    return p0 + lane_pair(p1, 1) + lane_pair(p2, 2)
+        return (pltpu.roll(t, step, 0) + pltpu.roll(t, window - step, 0))[mid]
+
+    result = []
+    for k in range(count):
+        x0, x1, x2 = f[k + 2], f[k + 1] + f[k + 3], f[k] + f[k + 4]
+        q0 = x0[mid]
+        q1 = x1[mid] + pair(x0, 1)
+        q2 = pair(x1, 1)
+        q4 = x2[mid] + pair(x0, 2)
+        q5 = pair(x2, 1) + pair(x1, 2)
+        p0, p1, p2 = layer_classes(q0, q1, q2, q4, q5)
+        result.append(p0 + lane_pair(p1, 1) + lane_pair(p2, 2))
+    return result
 
 
 def present(position, total, step):
@@ -57,7 +64,7 @@
 
 
 def weight_tile(layer, layers, row, rows, depth):
-    shape = (8, depth)
+    shape = (TALL, depth)
     sub = lax.broadcasted_iota(jnp.int32, shape, 0) + row
     spot = jnp.full(shape, layer, jnp.int32)
     nx1, nx2 = present(spot, layers, 1), present(spot, layers, 2)
@@ -68,21 +75,22 @@
     return p0 + present(lane, depth, 1) * p1 + present(lane, depth, 2) * p2
 
 
-def node_modes(ref, comp, layer, row):
-    t = ref[comp, layer, pl.ds(row, 16), :]
-    depth = t.shape[-1]
-    tn = jnp.where(lane_index(t.shape) < depth - 1, pltpu.roll(t, depth - 1, 1), 0.0)
-    s, d = t + tn, tn - t
-    s0, d0 = s[0:8], d[0:8]
-    s1, d1 = pltpu.roll(s, 15, 0)[0:8], pltpu.roll(d, 15, 0)[0:8]
-    return s0 + s1, d0 + d1, s1 - s0, d1 - d0
-
-
-def energy_tile(ref, layer, row):
+def node_modes(ref, layer, row):
+    result = []
+    for comp in range(3):
+        t = ref[comp, layer, pl.ds(row, SHORT + 8), :]
+        depth, window = t.shape[-1], t.shape[0]
+        tn = jnp.where(lane_index(t.shape) < depth - 1, pltpu.roll(t, depth - 1, 1), 0.0)
+        s, d = t + tn, tn - t
+        s0, d0 = s[0:SHORT], d[0:SHORT]
+        s1, d1 = pltpu.roll(s, window - 1, 0)[0:SHORT], pltpu.roll(d, window - 1, 0)[0:SHORT]
+        result.append((s0 + s1, d0 + d1, s1 - s0, d1 - d0))
+    return result
+
+
+def energy_tile(lower, upper):
     modes = []
-    for comp in range(3):
-        a = node_modes(ref, comp, layer, row)
-        b = node_modes(ref, comp, layer + 1, row)
+    for a, b in zip(lower, upper):
         modes.append(
             {
                 "x": b[0] - a[0],
@@ -115,12 +123,11 @@
 
 def kernel(
     ratio, density, void, fixed, disp, out,
-    moved, fix, col_s, col_r, cor_s, cor_r, dens, dead, scale, energy, other, sens, grad,
+    moved, fix, col_s, col_r, cor_s, cor_r, dens, dead, scale, energy, other, sens,
     local, send, recv,
 ):
     layers, rows, depth = density.shape
     half = layers // 2
-    tiles = rows // 8
     r, c, h = lax.axis_index("gz"), lax.axis_index("gy"), lax.axis_index("lc")
     nr, nc = lax.axis_size("gz"), lax.axis_size("gy")
     dz = 1 - 2 * h
@@ -154,15 +161,18 @@
     l0, b0 = half // 2 * (1 - h), half // 2 * h
     keep = half + 2
     lz, sb = (half + 2) * h, (layers - 2) * (1 - h)
+    plane, others = pl.ds(0, rows), pl.ds(1, layers - 1)
+    get_disp0 = pltpu.make_async_copy(disp.at[0, :, 0], moved.at[:, 0, plane, :], local.at[0])
+    get_fix0 = pltpu.make_async_copy(fixed.at[0], fix.at[0], local.at[1])
     get_disp = pltpu.make_async_copy(
-        disp.at[0], moved.at[:, pl.ds(0, layers), pl.ds(0, rows), :], local.at[0]
-    )
-    get_fix = pltpu.make_async_copy(fixed, fix, local.at[1])
+        disp.at[0, :, others], moved.at[:, others, plane, :], local.at[2]
+    )
+    get_fix = pltpu.make_async_copy(fixed.at[others], fix.at[others], local.at[3])
     get_dens = pltpu.make_async_copy(
-        density.at[pl.ds(b0, keep)], dens.at[pl.ds(l0, keep), mid, :], local.at[2]
-    )
-    get_dead = pltpu.make_async_copy(void.at[pl.ds(half * h, half)], dead, local.at[3])
-    for copy in (get_disp, get_fix, get_dens, get_dead):
+        density.at[pl.ds(b0, keep)], dens.at[pl.ds(l0, keep), mid, :], local.at[4]
+    )
+    get_dead = pltpu.make_async_copy(void.at[pl.ds(half * h, half)], dead, local.at[5])
+    for copy in (get_disp0, get_fix0, get_disp, get_fix, get_dens, get_dead):
         copy.start()
 
     barrier = pltpu.get_barrier_semaphore()
@@ -183,7 +193,6 @@
 
     span_z = 1 + (r > 0).astype(jnp.int32) + (r < nr - 1).astype(jnp.int32)
     span_y = 1 + (c > 0).astype(jnp.int32) + (c < nc - 1).astype(jnp.int32)
-    pl.semaphore_wait(barrier, 2 * span_z * span_y - 1)
 
     own, edge = pl.ds(b0, keep), pl.ds(sb, 2)
     top, bottom = pl.ds(rows - 8, 8), pl.ds(0, 8)
@@ -196,28 +205,32 @@
         remote(4, density.at[edge, bottom, :], dens.at[far, high, :], dz, -1, h),
     ]
 
-    get_disp.wait()
-    get_fix.wait()
-
     def free_layer(i, _):
         free = (1 - fix[i]).astype(jnp.float32)
         for comp in range(3):
-            moved[comp, i, pl.ds(0, rows), :] = moved[comp, i, pl.ds(0, rows), :] * free
+            moved[comp, i, plane, :] = moved[comp, i, plane, :] * free
         return 0
 
-    lax.fori_loop(0, layers, free_layer, 0)
+    send_layer = remote(
+        5, moved.at[:, 0, plane, :], moved.at[:, layers, plane, :], -1, 0, h
+    )
+    send_col = remote(6, col_s, col_r, 0, -1, h)
+    send_cor = remote(7, cor_s, cor_r, -1, -1, h)
+    get_disp0.wait()
+    get_fix0.wait()
+    free_layer(0, 0)
+    for comp in range(3):
+        cor_s[comp : comp + 1, :] = moved[comp, 0, 0:1, :]
+    pl.semaphore_wait(barrier, 2 * span_z * span_y - 1)
+    start(send_layer)
+    start(send_cor)
+    get_disp.wait()
+    get_fix.wait()
+    lax.fori_loop(1, layers, free_layer, 0)
     for comp in range(3):
         for i in range(layers):
             col_s[comp, i : i + 1, :] = moved[comp, i, 0:1, :]
-        cor_s[comp : comp + 1, :] = moved[comp, 0, 0:1, :]
-    plane = pl.ds(0, rows)
-    send_layer = remote(
-        5, moved.at[:, 0, plane, :], moved.at[:, layers, plane, :], -1, 0, h
-    )
-    send_col = remote(6, col_s, col_r, 0, -1, h)
-    send_cor = remote(7, cor_s, cor_r, -1, -1, h)
-    for entry in (send_col, send_cor, send_layer):
-        start(entry)
+    start(send_col)
     for entry in dens_copies:
         start(entry)
 
@@ -264,17 +277,17 @@
         (8, depth), ratio_sum.astype(jnp.float32)
     )
 
-    def energy_layer(i):
+    def energy_layers(first, count):
         def tile(j, _):
-            row = pl.multiple_of(j * 8, 8)
-            energy[i, pl.ds(row, 8), :] = share * energy_tile(moved, i, row)
+            row = pl.multiple_of(j * SHORT, SHORT)
+            lower = node_modes(moved, first, row)
+            for k in range(count):
+                upper = node_modes(moved, first + k + 1, row)
+                energy[first + k, pl.ds(row, SHORT), :] = share * energy_tile(lower, upper)
+                lower = upper
             return 0
 
-        lax.fori_loop(0, tiles, tile, 0)
-
-    def energy_step(k, _):
-        energy_layer(lax.rem(k + half * (1 - h), layers - 1))
-        return 0
+        lax.fori_loop(0, rows // SHORT, tile, 0)
 
     give = half * (1 - h)
     swap_a = remote(
@@ -283,90 +296,114 @@
     swap_b = remote(
         9, energy.at[pl.ds(give + half - 1, 1)], other.at[pl.ds(half - 1, 1)], 0, 0, 1 - h
     )
-    lax.fori_loop(0, half - 1, energy_step, 0)
+    energy_layers(give, half - 1)
     start(swap_a)
-    lax.fori_loop(half - 1, half, energy_step, 0)
+    energy_layers((half - 1) * h, half)
     pl.when(h == 1)(swap_b[0].start)
-    lax.fori_loop(half, layers - 1, energy_step, 0)
+
+    close, wide = 2 * (1 - h), 2 * h
+
+    def scale_two(j):
+        def tile(k, _):
+            row = pl.multiple_of(k * TALL, TALL)
+            cones = cone_tiles(dens, j, row, 2)
+            for n in range(2):
+                weights = weight_tile(
+                    r * layers + half * h + j + n, nr * layers, c * rows + row, nc * rows, depth
+                )
+                inverse = 1.0 / weights
+                physical = cones[n] * inverse
+                alive = (1 - dead[j + n, pl.ds(row, TALL), :]).astype(jnp.float32)
+                scale[j + n, pl.ds(row, TALL), :] = (
+                    alive * (-3.0 * (1.0 - 0.001)) * physical * physical * inverse
+                )
+            return 0
+
+        lax.fori_loop(0, rows // TALL, tile, 0)
+
+    def sense_two(j):
+        for n in range(2):
+            sens[2 + j + n, mid, :] = scale[j + n] * (energy[half * h + j + n] + other[j + n])
 
     get_dens.wait()
     get_dead.wait()
-    for entry in dens_copies:
-        arrive(entry)
-
-    def scale_step(n, _):
-        j, k = n // tiles, lax.rem(n, tiles)
-        row = pl.multiple_of(k * 8, 8)
-        weights = weight_tile(
-            r * layers + half * h + j, nr * layers, c * rows + row, nc * rows, depth
-        )
-        inverse = 1.0 / weights
-        physical = cone_tile(dens, j, row) * inverse
-        alive = (1 - dead[j, pl.ds(row, 8), :]).astype(jnp.float32)
-        scale[j, pl.ds(row, 8), :] = (
-            alive * (-3.0 * (1.0 - 0.001)) * physical * physical * inverse
-        )
-        return 0
-
-    lax.fori_loop(0, half * tiles, scale_step, 0)
+    arrive(dens_copies[1])
+    arrive(dens_copies[2])
+    scale_two(close)
+    arrive(swap_a)
+    pl.when(h == 0)(swap_b[0].wait_recv)
+    sense_two(close)
+
+    ps, pd = pl.ds(half - (half - 2) * h, 2), pl.ds((half + 2) * h, 2)
+    zs, zd = pl.ds(2 + (half - 2) * h, 2), pl.ds((half + 2) * (1 - h), 2)
+    last, first = pl.ds(rows, 8), pl.ds(8, 8)
+    close_copies = [
+        remote(10, sens.at[ps, mid, :], sens.at[pd, mid, :], 0, 0, 1 - h),
+        remote(12, sens.at[ps, last, :], sens.at[ps, low, :], 0, 1, h),
+        remote(13, sens.at[ps, first, :], sens.at[ps, high, :], 0, -1, h),
+        remote(14, sens.at[ps, last, :], sens.at[pd, low, :], 0, 1, 1 - h),
+        remote(15, sens.at[ps, first, :], sens.at[pd, high, :], 0, -1, 1 - h),
+    ]
+    for entry in close_copies:
+        start(entry)
 
     arrive(send_layer)
     arrive(send_cor)
     for comp in range(3):
         moved[comp, layers, pl.ds(rows, 1), :] = cor_r[comp : comp + 1, :]
-    energy_layer(layers - 1)
+    energy_layers(layers - 1, 1)
     pl.when(h == 0)(swap_b[0].start)
-    arrive(swap_a)
-    arrive(swap_b)
-
-    def sense_step(j, _):
-        sens[2 + j, mid, :] = scale[j] * (energy[half * h + j] + other[j])
-        return 0
-
-    lax.fori_loop(0, half, sense_step, 0)
-    ps, pd = pl.ds(half - (half - 2) * h, 2), pl.ds((half + 2) * h, 2)
-    zs, zd = pl.ds(2 + (half - 2) * h, 2), pl.ds((half + 2) * (1 - h), 2)
-    rest = pl.ds(2, half)
-    last, first = pl.ds(rows, 8), pl.ds(8, 8)
-    sense_copies = [
-        remote(11, sens.at[zs, mid, :], sens.at[zd, mid, :], -dz, 0, 1 - h),
-        remote(10, sens.at[ps, mid, :], sens.at[pd, mid, :], 0, 0, 1 - h),
-        remote(16, sens.at[zs, last, :], sens.at[zd, low, :], -dz, 1, 1 - h),
-        remote(17, sens.at[zs, first, :], sens.at[zd, high, :], -dz, -1, 1 - h),
-        remote(12, sens.at[rest, last, :], sens.at[rest, low, :], 0, 1, h),
-        remote(13, sens.at[rest, first, :], sens.at[rest, high, :], 0, -1, h),
-        remote(14, sens.at[ps, last, :], sens.at[pd, low, :], 0, 1, 1 - h),
-        remote(15, sens.at[ps, first, :], sens.at[pd, high, :], 0, -1, 1 - h),
+    for n in (0, 3, 4):
+        arrive(dens_copies[n])
+    scale_two(wide)
+    pl.when(h == 1)(swap_b[0].wait_recv)
+    sense_two(wide)
+
+    def flipped(index, src, dst, step_y):
+        copy, goes, _ = remote(index, src, dst, -dz, step_y, 1 - h)
+        return copy, goes, there(-dz, -step_y)
+
+    wide_copies = [
+        flipped(11, sens.at[zs, mid, :], sens.at[zd, mid, :], 0),
+        flipped(16, sens.at[zs, last, :], sens.at[zd, low, :], 1),
+        flipped(17, sens.at[zs, first, :], sens.at[zd, high, :], -1),
     ]
-    sides = {11: (-dz, 0), 16: (-dz, -1), 17: (-dz, 1)}
-    numbers = (11, 10, 16, 17, 12, 13, 14, 15)
-    sense_copies = [
-        (copy, goes, there(*sides[n]) if n in sides else comes)
-        for n, (copy, goes, comes) in zip(numbers, sense_copies)
+    row_copies = [
+        remote(18, sens.at[zs, last, :], sens.at[zs, low, :], 0, 1, h),
+        remote(19, sens.at[zs, first, :], sens.at[zs, high, :], 0, -1, h),
     ]
-    for entry in sense_copies:
+    for entry in wide_copies + row_copies:
         start(entry)
-    for entry in sense_copies:
+
+    def filter_two(j):
+        def tile(k, _):
+            row = pl.multiple_of(k * TALL, TALL)
+            cones = cone_tiles(sens, j, row, 2)
+            for n in range(2):
+                alive = (1 - dead[j + n, pl.ds(row, TALL), :]).astype(jnp.float32)
+                out[half * h + j + n, pl.ds(row, TALL), :] = alive * cones[n]
+            return 0
+
+        lax.fori_loop(0, rows // TALL, tile, 0)
+
+    def hand_over(index, j):
+        place = pl.ds(half * h + j, 2)
+        return remote(index, out.at[place], out.at[place], 0, 0, 1 - h)
+
+    for entry in close_copies + row_copies:
         arrive(entry)
-
-    def filter_step(n, _):
-        j, k = n // tiles, lax.rem(n, tiles)
-        row = pl.multiple_of(k * 8, 8)
-        alive = (1 - dead[j, pl.ds(row, 8), :]).astype(jnp.float32)
-        grad[j, pl.ds(row, 8), :] = alive * cone_tile(sens, j, row)
-        return 0
-
-    lax.fori_loop(0, half * tiles, filter_step, 0)
-    place = pl.ds(half * h, half)
-    put = pltpu.make_async_copy(grad, out.at[place], local.at[4])
-    give_out = remote(18, grad, out.at[place], 0, 0, 1 - h)
-    start(give_out)
-    put.start()
-    for entry in [*dens_copies, send_layer, send_col, send_cor, swap_a, swap_b, *sense_copies]:
+    filter_two(close)
+    give_close, give_wide = hand_over(20, close), hand_over(21, wide)
+    start(give_close)
+    for entry in wide_copies:
+        arrive(entry)
+    filter_two(wide)
+    start(give_wide)
+    sent = [*dens_copies, send_layer, send_col, send_cor, swap_a, swap_b]
+    for entry in sent + close_copies + wide_copies + row_copies + [give_close, give_wide]:
         left(entry)
-    left(give_out)
-    arrive(give_out)
-    put.wait()
+    arrive(give_close)
+    arrive(give_wide)
 
 
 def shards(density, void_mask, fixed_mask, displacement, load_ratio):
@@ -376,9 +413,9 @@
     hbm = pl.BlockSpec(memory_space=pl.ANY)
     return pl.pallas_call(
         kernel,
-        out_shape=jax.ShapeDtypeStruct(density.shape, f32),
+        out_shape=pltpu.VMEM(density.shape, f32),
         in_specs=[pl.BlockSpec(memory_space=pltpu.SMEM), hbm, hbm, hbm, hbm],
-        out_specs=hbm,
+        out_specs=pl.BlockSpec(memory_space=pltpu.VMEM),
         scratch_shapes=[
             pltpu.VMEM((3, layers + 1, rows + 8, depth), f32),
             pltpu.VMEM((layers, rows, depth), jnp.int32),
@@ -392,8 +429,7 @@
             pltpu.VMEM((layers, rows, depth), f32),
             pltpu.VMEM((half, rows, depth), f32),
             pltpu.VMEM((half + 4, rows + 16, depth), f32),
-            pltpu.VMEM((half, rows, depth), f32),
-            pltpu.SemaphoreType.DMA((5,)),
+            pltpu.SemaphoreType.DMA((6,)),
             pltpu.SemaphoreType.DMA((N_COPIES,)),
             pltpu.SemaphoreType.DMA((N_COPIES,)),
         ],

time: 30 us -> 21.1 us (0.70)
  Pallas kernels: 27.9 us -> 20.1 us
  local copies, waits for them, and re-layouts: 1.87 us -> 0.8 us
    pallas_call x1, Pallas kernels: 27.9 us -> 20.1 us  [shards(): pl.pallas_call(kernel, out_shape=pltpu.VMEM(density.shape, f32), in_specs...]
    unnamed x1, local copies, waits for them, and re-layouts: 1.87 us -> 0.8 us
where the time goes in v2:
time: 21.1 us; the launch traced here: 20.9 us
  Pallas kernels  20.1 us (95%)
  local copies, waits for them, and re-layouts  0.8 us (4%)
    pallas_call x1, Pallas kernels, shards(): pl.pallas_call(kernel, out_shape=pltpu.VMEM(density.shape, f32), in_specs...  20.1 us
    unnamed x1, local copies, waits for them, and re-layouts  0.8 us

profile of v2, /device:TPU:0, one launch (start us, length us, event | category | flops | bytes accessed | tf_op | source)
XLA Modules:
  0.0 20.9 jit_solution(17630376643454990289)
XLA Ops:
  0.0 20.1 %shard_map.55 = f32[8,64,256]{2,1,0:T(8,128)S(1)} custom-call(s32[2]{0:T(128)} %ratio.1, f32[8,64,256]{2,1,0:T(8,128)} %density.1, s32[8,64,256]{2,1,0:T(8,128)} %void.1, s32[8,64,256]{2,1,0:T(8,128)} %fixed.1, f32[1,3,8,64,256]{4,3,2,1,0:T(8,128)} %disp.1), custom_call_target="tpu_custom_call" | custom-call | tf_op jit(solution)/shard_map/pallas_call | solution.py:414
  20.1 0.8 %copy.7 = f32[8,64,256]{2,1,0:T(8,128)} copy(f32[8,64,256]{2,1,0:T(8,128)S(1)} %shard_map.55) | data formatting | bytes 1048576

commit v3 on v2

--- a/solution.py
+++ b/solution.py
@@ -13,8 +13,9 @@
 LAMBDA = POISSON * FACTOR
 SHEAR = (0.5 - POISSON) * FACTOR
 W = [2.5 - math.sqrt(d) for d in range(7)]
-N_COPIES = 24
-TALL = 16
+N_COPIES = 40
+CHUNKS = 4
+TALL = 32
 SHORT = 8
 
 
@@ -123,7 +124,7 @@
 
 def kernel(
     ratio, density, void, fixed, disp, out,
-    moved, fix, col_s, col_r, cor_s, cor_r, dens, dead, scale, energy, other, sens,
+    moved, extra, fix, col_s, col_r, cor_s, cor_r, cor_x, dens, dead, scale, energy, other, sens,
     local, send, recv,
 ):
     layers, rows, depth = density.shape
@@ -146,6 +147,10 @@
         goes, comes = there(step_z, step_y), there(-step_z, -step_y)
         return copy, goes, comes
 
+    def between(index, src, dst, step_z, step_y, giver, taker):
+        copy, goes, comes = remote(index, src, dst, step_z, step_y, taker)
+        return copy, goes & (h == giver), comes & (h == taker)
+
     def start(entry):
         copy, goes, _ = entry
         pl.when(goes)(copy.start)
@@ -211,19 +216,31 @@
             moved[comp, i, plane, :] = moved[comp, i, plane, :] * free
         return 0
 
-    send_layer = remote(
-        5, moved.at[:, 0, plane, :], moved.at[:, layers, plane, :], -1, 0, h
-    )
+    tall = rows // CHUNKS
+    chunks = [pl.ds(q * tall, tall) for q in range(CHUNKS)]
+    first_layer = [
+        [
+            between(24 + q, moved.at[:, 0, part, :], extra.at[:, 1, part, :], -1, 0, 0, 1),
+            between(28 + q, moved.at[:, 0, part, :], moved.at[:, layers, part, :], -1, 0, 1, 1),
+        ]
+        for q, part in enumerate(chunks)
+    ]
     send_col = remote(6, col_s, col_r, 0, -1, h)
-    send_cor = remote(7, cor_s, cor_r, -1, -1, h)
+    send_cor = [
+        between(7, cor_s, cor_r, -1, -1, 1, 1),
+        between(5, cor_s, cor_x, -1, -1, 0, 1),
+    ]
     get_disp0.wait()
     get_fix0.wait()
     free_layer(0, 0)
     for comp in range(3):
         cor_s[comp : comp + 1, :] = moved[comp, 0, 0:1, :]
     pl.semaphore_wait(barrier, 2 * span_z * span_y - 1)
-    start(send_layer)
-    start(send_cor)
+    for entry in [*send_cor, *first_layer[-1], dens_copies[0]]:
+        start(entry)
+    for pieces in first_layer[-2::-1]:
+        for entry in pieces:
+            start(entry)
     get_disp.wait()
     get_fix.wait()
     lax.fori_loop(1, layers, free_layer, 0)
@@ -231,13 +248,14 @@
         for i in range(layers):
             col_s[comp, i : i + 1, :] = moved[comp, i, 0:1, :]
     start(send_col)
-    for entry in dens_copies:
+    for entry in dens_copies[1:]:
         start(entry)
 
     @pl.when(r == nr - 1)
     def _():
         for comp in range(3):
             moved[comp, layers, plane, :] = jnp.zeros((rows, depth), jnp.float32)
+            extra[comp, 1, plane, :] = jnp.zeros((rows, depth), jnp.float32)
 
     @pl.when(c == nc - 1)
     def _():
@@ -246,6 +264,7 @@
     @pl.when(jnp.logical_not(there(1, 1)))
     def _():
         cor_r[...] = jnp.zeros_like(cor_r)
+        cor_x[...] = jnp.zeros_like(cor_x)
 
     blank = jnp.zeros((8, depth), jnp.float32)
     for ref in (dens, sens):
@@ -270,12 +289,17 @@
         for i in range(layers):
             moved[comp, i, pl.ds(rows, 1), :] = col_r[comp, i : i + 1, :]
 
+    send_own = between(
+        23, moved.at[:, layers - 1], extra.at[:, 0], 0, 0, 0, 1
+    )
+    start(send_own)
+
     ratio_sum = ratio[0]
     for case in range(1, ratio.shape[0]):
         ratio_sum = ratio_sum + ratio[case]
-    share = jnp.full((8, depth), ratio[h].astype(jnp.float32)) / jnp.full(
-        (8, depth), ratio_sum.astype(jnp.float32)
-    )
+    total = jnp.full((8, depth), ratio_sum.astype(jnp.float32))
+    share = jnp.full((8, depth), ratio[h].astype(jnp.float32)) / total
+    share_x = jnp.full((8, depth), ratio[1 - h].astype(jnp.float32)) / total
 
     def energy_layers(first, count):
         def tile(j, _):
@@ -293,13 +317,13 @@
     swap_a = remote(
         8, energy.at[pl.ds(give, half - 1)], other.at[pl.ds(0, half - 1)], 0, 0, 1 - h
     )
-    swap_b = remote(
-        9, energy.at[pl.ds(give + half - 1, 1)], other.at[pl.ds(half - 1, 1)], 0, 0, 1 - h
+    swap_b = between(
+        9, energy.at[pl.ds(half - 1, 1)], other.at[pl.ds(half - 1, 1)], 0, 0, 1, 0
     )
     energy_layers(give, half - 1)
     start(swap_a)
     energy_layers((half - 1) * h, half)
-    pl.when(h == 1)(swap_b[0].start)
+    start(swap_b)
 
     close, wide = 2 * (1 - h), 2 * h
 
@@ -321,9 +345,8 @@
 
         lax.fori_loop(0, rows // TALL, tile, 0)
 
-    def sense_two(j):
-        for n in range(2):
-            sens[2 + j + n, mid, :] = scale[j + n] * (energy[half * h + j + n] + other[j + n])
+    def sense(j):
+        sens[2 + j, mid, :] = scale[j] * (energy[half * h + j] + other[j])
 
     get_dens.wait()
     get_dead.wait()
@@ -331,8 +354,9 @@
     arrive(dens_copies[2])
     scale_two(close)
     arrive(swap_a)
-    pl.when(h == 0)(swap_b[0].wait_recv)
-    sense_two(close)
+    arrive(swap_b)
+    sense(close)
+    sense(close + 1)
 
     ps, pd = pl.ds(half - (half - 2) * h, 2), pl.ds((half + 2) * h, 2)
     zs, zd = pl.ds(2 + (half - 2) * h, 2), pl.ds((half + 2) * (1 - h), 2)
@@ -347,24 +371,60 @@
     for entry in close_copies:
         start(entry)
 
-    arrive(send_layer)
-    arrive(send_cor)
-    for comp in range(3):
-        moved[comp, layers, pl.ds(rows, 1), :] = cor_r[comp : comp + 1, :]
-    energy_layers(layers - 1, 1)
-    pl.when(h == 0)(swap_b[0].start)
     for n in (0, 3, 4):
         arrive(dens_copies[n])
     scale_two(wide)
-    pl.when(h == 1)(swap_b[0].wait_recv)
-    sense_two(wide)
+    sense(wide)
+    below = between(11, sens.at[pl.ds(2, 2), mid, :], sens.at[pl.ds(half + 2, 2), mid, :], -1, 0, 0, 1)
+    above = between(22, sens.at[half, mid, :], sens.at[0, mid, :], 1, 0, 1, 0)
+    last_layer = [
+        between(
+            32 + q,
+            sens.at[half + 1, pl.ds(8 + q * tall, tall), :],
+            sens.at[1, pl.ds(8 + q * tall, tall), :],
+            1, 0, 1, 0,
+        )
+        for q in range(CHUNKS)
+    ]
+    start(above)
+
+    @pl.when(h == 0)
+    def _():
+        sense(1)
+
+    start(below)
+
+    @pl.when(h == 1)
+    def _():
+        for entry in [*send_cor, send_own]:
+            arrive(entry)
+        for comp in range(3):
+            moved[comp, layers, pl.ds(rows, 1), :] = cor_r[comp : comp + 1, :]
+            extra[comp, 1, pl.ds(rows, 1), :] = cor_x[comp : comp + 1, :]
+        for q in reversed(range(CHUNKS)):
+            for entry in first_layer[q]:
+                arrive(entry)
+
+            def tile(k, _):
+                row = pl.multiple_of(q * tall + k * SHORT, SHORT)
+                here = pl.ds(row, SHORT)
+                own = energy_tile(
+                    node_modes(moved, layers - 1, row), node_modes(moved, layers, row)
+                )
+                his = energy_tile(node_modes(extra, 0, row), node_modes(extra, 1, row))
+                sens[half + 1, pl.ds(row + 8, SHORT), :] = scale[half - 1, here, :] * (
+                    share * own + share_x * his
+                )
+                return 0
+
+            lax.fori_loop(0, tall // SHORT, tile, 0)
+            start(last_layer[q])
 
     def flipped(index, src, dst, step_y):
         copy, goes, _ = remote(index, src, dst, -dz, step_y, 1 - h)
         return copy, goes, there(-dz, -step_y)
 
     wide_copies = [
-        flipped(11, sens.at[zs, mid, :], sens.at[zd, mid, :], 0),
         flipped(16, sens.at[zs, last, :], sens.at[zd, low, :], 1),
         flipped(17, sens.at[zs, first, :], sens.at[zd, high, :], -1),
     ]
@@ -374,6 +434,7 @@
     ]
     for entry in wide_copies + row_copies:
         start(entry)
+    wide_copies = [below, above, *last_layer, *wide_copies]
 
     def filter_two(j):
         def tile(k, _):
@@ -399,7 +460,9 @@
         arrive(entry)
     filter_two(wide)
     start(give_wide)
-    sent = [*dens_copies, send_layer, send_col, send_cor, swap_a, swap_b]
+    sent = [*dens_copies, send_col, *send_cor, swap_a, swap_b, send_own]
+    for pieces in first_layer:
+        sent.extend(pieces)
     for entry in sent + close_copies + wide_copies + row_copies + [give_close, give_wide]:
         left(entry)
     arrive(give_close)
@@ -418,9 +481,11 @@
         out_specs=pl.BlockSpec(memory_space=pltpu.VMEM),
         scratch_shapes=[
             pltpu.VMEM((3, layers + 1, rows + 8, depth), f32),
+            pltpu.VMEM((3, 2, rows + 8, depth), f32),
             pltpu.VMEM((layers, rows, depth), jnp.int32),
             pltpu.VMEM((3, layers, depth), f32),
             pltpu.VMEM((3, layers, depth), f32),
+            pltpu.VMEM((8, depth), f32),
             pltpu.VMEM((8, depth), f32),
             pltpu.VMEM((8, depth), f32),
             pltpu.VMEM((half + 4, rows + 16, depth), f32),

time: 21.1 us -> 20.6 us (0.976)
  Pallas kernels: 20.1 us -> 19.6 us
    pallas_call x1, Pallas kernels: 20.1 us -> 19.6 us  [shards(): pl.pallas_call(kernel, out_shape=pltpu.VMEM(density.shape, f32), in_specs...]
where the time goes in v3:
time: 20.6 us; the launch traced here: 20.4 us
  Pallas kernels  19.6 us (95%)
  local copies, waits for them, and re-layouts  0.8 us (4%)
    pallas_call x1, Pallas kernels, shards(): pl.pallas_call(kernel, out_shape=pltpu.VMEM(density.shape, f32), in_specs...  19.6 us
    unnamed x1, local copies, waits for them, and re-layouts  0.8 us

profile of v3, /device:TPU:0, one launch (start us, length us, event | category | flops | bytes accessed | tf_op | source)
XLA Modules:
  0.0 20.4 jit_solution(6526339781996055460)
XLA Ops:
  0.0 19.6 %shard_map.55 = f32[8,64,256]{2,1,0:T(8,128)S(1)} custom-call(s32[2]{0:T(128)} %ratio.1, f32[8,64,256]{2,1,0:T(8,128)} %density.1, s32[8,64,256]{2,1,0:T(8,128)} %void.1, s32[8,64,256]{2,1,0:T(8,128)} %fixed.1, f32[1,3,8,64,256]{4,3,2,1,0:T(8,128)} %disp.1), custom_call_target="tpu_custom_call" | custom-call | tf_op jit(solution)/shard_map/pallas_call | solution.py:477
  19.6 0.8 %copy.7 = f32[8,64,256]{2,1,0:T(8,128)} copy(f32[8,64,256]{2,1,0:T(8,128)S(1)} %shard_map.55) | data formatting | bytes 1048576

commit v4 on v3

--- a/solution.py
+++ b/solution.py
@@ -14,7 +14,7 @@
 SHEAR = (0.5 - POISSON) * FACTOR
 W = [2.5 - math.sqrt(d) for d in range(7)]
 N_COPIES = 40
-CHUNKS = 4
+CHUNKS = 2
 TALL = 32
 SHORT = 8
 
@@ -236,7 +236,7 @@
     for comp in range(3):
         cor_s[comp : comp + 1, :] = moved[comp, 0, 0:1, :]
     pl.semaphore_wait(barrier, 2 * span_z * span_y - 1)
-    for entry in [*send_cor, *first_layer[-1], dens_copies[0]]:
+    for entry in [*send_cor, *first_layer[-1]]:
         start(entry)
     for pieces in first_layer[-2::-1]:
         for entry in pieces:
@@ -248,7 +248,7 @@
         for i in range(layers):
             col_s[comp, i : i + 1, :] = moved[comp, i, 0:1, :]
     start(send_col)
-    for entry in dens_copies[1:]:
+    for entry in dens_copies:
         start(entry)
 
     @pl.when(r == nr - 1)

time: 20.6 us -> 20.5 us (level)
  no operation moved by 1% of the time
where the time goes in v4:
time: 20.5 us; the launch traced here: 20.4 us
  Pallas kernels  19.6 us (96%)
  local copies, waits for them, and re-layouts  0.8 us (4%)
    pallas_call x1, Pallas kernels, shards(): pl.pallas_call(kernel, out_shape=pltpu.VMEM(density.shape, f32), in_specs...  19.6 us
    unnamed x1, local copies, waits for them, and re-layouts  0.8 us

profile of v4, /device:TPU:0, one launch (start us, length us, event | category | flops | bytes accessed | tf_op | source)
XLA Modules:
  0.0 20.4 jit_solution(8001676157976221889)
XLA Ops:
  0.0 19.6 %shard_map.55 = f32[8,64,256]{2,1,0:T(8,128)S(1)} custom-call(s32[2]{0:T(128)} %ratio.1, f32[8,64,256]{2,1,0:T(8,128)} %density.1, s32[8,64,256]{2,1,0:T(8,128)} %void.1, s32[8,64,256]{2,1,0:T(8,128)} %fixed.1, f32[1,3,8,64,256]{4,3,2,1,0:T(8,128)} %disp.1), custom_call_target="tpu_custom_call" | custom-call | tf_op jit(solution)/shard_map/pallas_call | solution.py:477
  19.6 0.8 %copy.7 = f32[8,64,256]{2,1,0:T(8,128)} copy(f32[8,64,256]{2,1,0:T(8,128)S(1)} %shard_map.55) | data formatting | bytes 1048576
